TPU v7x, 128 devices: a whole 4x4x4 slice. The times are simulated.
128 devices in a mesh: dp: 8 (over z, core), mp: 16 (over y, x).
Axes of the slice: x: 4, y: 4, z: 4, core: 2. Of those that a mesh axis runs over, the one named last changes fastest.
Arguments:
- crop_hidden: bfloat16 [8, 1536, 8192], P(None, 'dp', 'mp'), may hold values from -15 to 15
- projector_weight: bfloat16 [8192, 8192], P('mp'), may hold values from -0.21213203 to 0.21213203
- pairing: int32 [8, 1536], P(None, 'dp'), may hold values from 0 to 191, as said below
Outputs:
- embeddings: float32 [8192, 8, 1536], P('mp', 'dp')
- loss_terms: float32 [4], replicated
Inputs may be any that keep to these rules, and one draw needn't show every extreme that they name: Each aligned block of 192 entries of a row of pairing is a permutation of 0 to 191.
All inputs are finite; a program needn't handle non-finite values.
Results may differ from a plain program's by a relative error of at most 0.0003.
Values may be sent and summed in bfloat16 or wider, within the bound.
No kernel may reach another device: no remote copies, remote signals or barrier semaphores. Data moves between devices by JAX's collectives and lax.ppermute only.
A program may use at most 128 MiB of HBM per device.

v0:
```python
import functools
import jax
import jax.numpy as jnp
from jax import lax
from jax.sharding import Mesh
from jax.sharding import PartitionSpec as P

MP = ("mp_0", "mp_1")
DP = ("dp_0", "dp_1")
DP_MP = ("dp_0", "dp_1", "mp_0", "mp_1")
highest = lax.Precision.HIGHEST
epsilon = 0.0001


def by_axis(x, axes):
    return functools.reduce(lax.psum, axes, x)


def local(crop_hidden, projector_weight, pairing):
    crop_count, local_rows, width_part = crop_hidden.shape
    features = projector_weight.shape[1]
    total_rows = crop_count * local_rows
    column_block = lax.all_to_all(projector_weight, MP, split_axis=1, concat_axis=0, tiled=True)
    shards = lax.all_gather(crop_hidden, MP, axis=2, tiled=True)
    flat_piece = shards.reshape(total_rows, shards.shape[2])
    embedded = lax.dot_general(
        column_block, flat_piece, (((0,), (1,)), ((), ())), preferred_element_type=jnp.float32
    )
    feature_part = embedded.shape[0]
    by_crop = embedded.reshape(feature_part, crop_count, local_rows)
    onehot = (pairing[:, :, None] == jnp.arange(local_rows, dtype=jnp.int32)[None, None, :]).astype(
        jnp.float32
    )
    aligned = jnp.einsum("jcr,cri->jci", by_crop, onehot, precision=highest)
    invariance = 0.0
    for anchor in range(2):
        differ = aligned - aligned[:, anchor : anchor + 1, :]
        invariance = invariance + jnp.sum(differ * differ)
    owned_block = lax.all_to_all(by_crop, DP, split_axis=1, concat_axis=2, tiled=True)
    batch_rows = owned_block.shape[2]
    column_mean = jnp.mean(owned_block, axis=2, keepdims=True)
    centered = owned_block - column_mean
    variance = jnp.sum(centered * centered, axis=2) / (batch_rows - 1)
    hinge_sum = jnp.sum(jax.nn.relu(1.0 - jnp.sqrt(variance + epsilon)))
    diagonal_sq = jnp.sum(variance * variance)
    gram_scale = 1.0 / ((batch_rows - 1) * (batch_rows - 1))
    partial_gram = jnp.einsum("jcr,jcs->crs", centered, centered, precision=highest)
    gram_block = lax.psum(partial_gram.astype(jnp.bfloat16), MP).astype(jnp.float32)
    frobenius = jnp.where(
        lax.axis_index(MP) == 0, jnp.sum(gram_block * gram_block) * gram_scale, 0.0
    )
    totals = (
        by_axis(invariance, DP_MP),
        by_axis(hinge_sum, DP_MP),
        by_axis(frobenius - diagonal_sq, DP_MP),
    )
    invariance_loss = totals[0] / (2 * (crop_count - 1) * batch_rows * features)
    variance_loss = totals[1] / (crop_count * features)
    covariance_loss = totals[2] / (crop_count * features)
    total_loss = 25.0 * invariance_loss + 25.0 * variance_loss + covariance_loss
    loss_terms = jnp.stack([invariance_loss, variance_loss, covariance_loss, total_loss])
    return (owned_block, loss_terms)


def solution(mesh):
    torus = Mesh(mesh.devices.reshape(4, 2, 4, 4), ("dp_0", "dp_1", "mp_0", "mp_1"))
    placed = (P(None, DP, MP), P(MP, None), P(None, DP))
    return jax.shard_map(
        local, mesh=torus, in_specs=placed, out_specs=(P(MP, DP, None), P()), check_vma=False
    )
```

profile of v0, /device:TPU:0, one launch (start us, length us, event | category | flops | bytes accessed | tf_op | source)
XLA Modules:
  0.0 498.9 jit_solution(17605152332946094416)
XLA Ops:
  7.2 0.7 all-gather.2.cloned.1.call-update
  7.9 0.0 all-reduce.6.cloned.1.call-start
  7.9 7.5 %copy.9 = bf16[64,16,8,512]{3,2,0,1:T(8,128)(2,1)} copy(bf16[64,16,8,512]{3,2,1,0:T(8,128)(2,1)} %bitcast.30) | data formatting | bytes 16777216 | tf_op jit(solution)/shard_map/all_to_all | solution.py:23
  15.4 128.3 %all_to_all.31 = bf16[512,16,512]{2,0,1:T(8,128)(2,1)} all-to-all(bf16[512,16,512]{2,0,1:T(8,128)(2,1)} %bitcast.29), channel_id=1, replica_groups=mesh['dp_0'=4,'dp_1'=2,'mp_0'=4,'mp_1'=4] {'mp_0','mp_1'}, dimensions={1} | all-to-all | bytes 16777216 | tf_op jit(solution)/shard_map/all_to_all | solution.py:23
  143.8 117.0 %all-gather.2.cloned.1.call-done = bf16[8,192,8192]{2,1,0:T(8,128)(2,1)} async-done(((bf16[8,192,512]{2,1,0:T(8,128)(2,1)}), bf16[8,192,8192]{2,1,0:T(8,128)(2,1)}) %all-gather.2.cloned.1.call-update) | async-done | bytes 25165840 | tf_op jit(solution)/shard_map/all_gather | solution.py:24
  260.8 18.9 %fusion.2 = f32[512,8,192]{0,2,1:T(8,128)S(1)} fusion(bf16[8192,512,1]{1,0,2:T(8,128)(2,1)} %bitcast.31, bf16[8,192,8192]{2,1,0:T(8,128)(2,1)} %all-gather.2.cloned.1.call-done), kind=kOutput, calls=%fused_computation.17 | convolution fusion | flops 12884901888 | bytes 36700160 | tf_op jit(solution)/shard_map/dot_general | solution.py:26
  279.7 1.7 copy-done
  281.3 42.7 %all_to_all.32 = f32[512,8,192]{0,2,1:T(8,128)S(1)} all-to-all(f32[512,8,192]{0,2,1:T(8,128)S(1)} %fusion.2), channel_id=1, replica_groups=mesh['dp_0'=4,'dp_1'=2,'mp_0'=4,'mp_1'=4] {'dp_0','dp_1'}, dimensions={1} | all-to-all | bytes 6291456 | tf_op jit(solution)/shard_map/all_to_all | solution.py:39
  324.0 0.3 reduce_sum.65
  324.3 0.6 multiply_reduce_fusion.1
  324.8 16.8 %fusion = bf16[1,1536,1536]{2,1,0:T(8,128)(2,1)} fusion(f32[512,1536]{0,1:T(8,128)S(1)} %bitcast.32), kind=kOutput, calls=%fused_computation.3 | convolution fusion | flops 14497873920 | bytes 7864320 | tf_op jit(solution)/shard_map/jcr,jcs->crs/dot_general | solution.py:47
  341.6 0.7 copy-done.1
  342.3 3.9 convolution_bitcast_fusion
  346.2 0.1 slice_bitcast_fusion.1
  346.2 2.0 multiply_reduce_fusion.2
  349.5 5.4 %copy.6 = f32[512,1,1536]{2,1,0:T(1,128)} copy(f32[512,1,1536]{0,2,1:T(8,128)S(1)} %bitcast.28) | data formatting | bytes 6291456
  354.9 0.7 multiply_reduce_fusion.4
  355.6 91.4 %all-reduce.6.cloned.1.call-done = bf16[1,1536,1536]{2,1,0:T(8,128)(2,1)} async-done(((bf16[1,1536,1536]{2,1,0:T(8,128)(2,1)}), bf16[1,1536,1536]{2,1,0:T(8,128)(2,1)}) %all-reduce.6.cloned.1.call-update) | async-done | bytes 4718608 | tf_op jit(solution)/shard_map/psum | solution.py:48
  447.0 5.3 %multiply_reduce_fusion = f32[]{:T(128)} fusion(bf16[1,1536,1536]{2,1,0:T(8,128)(2,1)} %all-reduce.6.cloned.1.call-done), kind=kLoop, calls=%fused_computation | loop fusion | flops 7077887 | bytes 4718596 | tf_op jit(solution)/shard_map/reduce_sum | solution.py:50
  453.5 11.3 %all-reduce.2 = (f32[]{:T(128)}, f32[]{:T(128)}, f32[]{:T(128)}) all-reduce(f32[]{:T(128)S(6)} %add.47, f32[]{:T(128)} %get-tuple-element.7, f32[]{:T(128)S(6)} %sub.61), channel_id=1, replica_groups=mesh['dp_0'=4,'dp_1'=2,'mp_0'=4,'mp_1'=4] {'dp_0'}, use_global_device_ids=true, to_apply=%region_2.0 | all-reduce | flops 3 | bytes 24 | tf_op jit(solution)/shard_map/psum | solution.py:16
  464.8 3.2 all-reduce.3
  467.9 11.0 %all-reduce.1 = (f32[]{:T(128)}, f32[]{:T(128)}, f32[]{:T(128)}) all-reduce(f32[]{:T(128)} %get-tuple-element.17, f32[]{:T(128)} %get-tuple-element.18, f32[]{:T(128)} %get-tuple-element.19), channel_id=1, replica_groups=mesh['dp_0'=4,'dp_1'=2,'mp_0'=4,'mp_1'=4] {'mp_0'}, use_global_device_ids=true, to_apply=%region_4.5 | all-reduce | flops 3 | bytes 24 | tf_op jit(solution)/shard_map/psum | solution.py:16
  478.9 9.4 %all-reduce = (f32[]{:T(128)}, f32[]{:T(128)}, f32[]{:T(128)}) all-reduce(f32[]{:T(128)} %get-tuple-element.11, f32[]{:T(128)} %get-tuple-element.12, f32[]{:T(128)} %get-tuple-element.13), channel_id=1, replica_groups=mesh['dp_0'=4,'dp_1'=2,'mp_0'=4,'mp_1'=4] {'mp_1'}, use_global_device_ids=true, to_apply=%region_5.6 | all-reduce | flops 3 | bytes 24 | tf_op jit(solution)/shard_map/psum | solution.py:16
  491.5 0.6 pad_maximum_fusion
  (5 shorter events, 0.1 us)
Async XLA Ops:
  7.2 253.6 %all-gather.2.cloned.1.call-start = ((), (), s32[]{:S(2)}) async-start(), calls=%async_computation.2 | async-start | bytes 26738688 | tf_op jit(solution)/shard_map/all_gather | solution.py:24
  7.9 439.1 %all-reduce.6.cloned.1.call-start = ((), (), s32[]{:S(2)}) async-start(), calls=%async_computation.3 | async-start | bytes 9437184 | tf_op jit(solution)/shard_map/psum | solution.py:48
  279.7 1.7 copy-start
  341.6 0.7 copy-start.1
Sparse Core Ops, SparseCore 0:
  10.1 250.6 all-gather.1
  341.7 105.2 all-reduce.5
where the time goes:
time: 499 us
  waiting for transfers between devices  209 us (42%)
  blocking collectives  206 us (41%)
  matrix products  39.5 us (8%)
  between operations  19.8 us (4%)
  local copies, waits for them, and re-layouts  15.3 us (3%)
  other arithmetic  9.4 us (2%)
    all_to_all x1, blocking collectives, local(): lax.all_to_all(projector_weight, MP, split_axis=1, concat_axis=0, tiled=T...  128 us
    all_gather x1, waiting for transfers between devices, local(): shards = lax.all_gather(crop_hidden, MP, axis=2, tiled=True)  117 us
    psum x1, waiting for transfers between devices, local(): lax.psum(partial_gram.astype(jnp.bfloat16), MP).astype(jnp.float32)  91.4 us
    all_to_all x1, blocking collectives, local(): lax.all_to_all(by_crop, DP, split_axis=1, concat_axis=2, tiled=True)  42.7 us
    psum x4, blocking collectives, by_axis(): return functools.reduce(lax.psum, axes, x)  34.8 us
    dot_general x1, matrix products, local(): lax.dot_general(column_block, flat_piece, (((0,), (1,)), ((), ())), prefe...  18.9 us
    dot_general x1, matrix products, local(): jnp.einsum('jcr,jcs->crs', centered, centered, precision=highest)  16.8 us
  transfers between devices with their start and end apart: 2, of which 2 were waited for; matrix products, arithmetic and copies ran while one was open for 4% of the time, Pallas kernels for 0%

commit v1 on v0

--- a/solution.py
+++ b/solution.py
@@ -4,12 +4,20 @@
 from jax import lax
 from jax.sharding import Mesh
 from jax.sharding import PartitionSpec as P
+from jax.lax import all_to_all, axis_size
 
 MP = ("mp_0", "mp_1")
 DP = ("dp_0", "dp_1")
 DP_MP = ("dp_0", "dp_1", "mp_0", "mp_1")
 highest = lax.Precision.HIGHEST
 epsilon = 0.0001
+
+
+def update_series_all(my_data):
+    cards = []
+    for _ in range(axis_size(MP)):
+        cards.append(my_data)
+    return jnp.concatenate(all_to_all(jnp.stack(cards), MP, 0, 0), axis=2)
 
 
 def by_axis(x, axes):
@@ -21,7 +29,7 @@
     features = projector_weight.shape[1]
     total_rows = crop_count * local_rows
     column_block = lax.all_to_all(projector_weight, MP, split_axis=1, concat_axis=0, tiled=True)
-    shards = lax.all_gather(crop_hidden, MP, axis=2, tiled=True)
+    shards = update_series_all(crop_hidden)
     flat_piece = shards.reshape(total_rows, shards.shape[2])
     embedded = lax.dot_general(
         column_block, flat_piece, (((0,), (1,)), ((), ())), preferred_element_type=jnp.float32

time: 499 us -> 656 us (1.31)
  blocking collectives: 206 us -> 462 us
  waiting for transfers between devices: 209 us -> 89.2 us
  local copies, waits for them, and re-layouts: 15.3 us -> 34.9 us
    all_to_all x0 -> x1, blocking collectives: none -> 281 us  [update_series_all(): return jnp.concatenate(all_to_all(jnp.stack(cards), MP, 0, 0), axis=2)]
    all_gather x1 -> x0, waiting for transfers between devices: 117 us -> none  [local(): shards = lax.all_gather(crop_hidden, MP, axis=2, tiled=True)]
    all_to_all x1, blocking collectives: 128 us -> 103 us  [local(): lax.all_to_all(projector_weight, MP, split_axis=1, concat_axis=0, tiled=T...]
    unnamed x5 -> x8, local copies, waits for them, and re-layouts: 7.75 us -> 19.7 us
  transfers between devices with their start and end apart: 2 -> 1, of which waited for: 2 -> 1; matrix products, arithmetic and copies ran while one was open for 4% -> 2% of each run, Pallas kernels for 0% -> 0%
where the time goes in v1:
time: 656 us; the launch traced here: 655 us
  blocking collectives  462 us (70%)
  waiting for transfers between devices  89.2 us (14%)
  matrix products  39.5 us (6%)
  local copies, waits for them, and re-layouts  34.9 us (5%)
  between operations  19.8 us (3%)
  other arithmetic  9.4 us (1%)
    all_to_all x1, blocking collectives, update_series_all(): return jnp.concatenate(all_to_all(jnp.stack(cards), MP, 0, 0), axis=2)  281 us
    all_to_all x1, blocking collectives, local(): lax.all_to_all(projector_weight, MP, split_axis=1, concat_axis=0, tiled=T...  103 us
    psum x1, waiting for transfers between devices, local(): lax.psum(partial_gram.astype(jnp.bfloat16), MP).astype(jnp.float32)  89.2 us
    all_to_all x1, blocking collectives, local(): lax.all_to_all(by_crop, DP, split_axis=1, concat_axis=2, tiled=True)  43.5 us
    psum x4, blocking collectives, by_axis(): return functools.reduce(lax.psum, axes, x)  34.8 us
    unnamed x8, local copies, waits for them, and re-layouts  19.7 us
    dot_general x1, matrix products, local(): lax.dot_general(column_block, flat_piece, (((0,), (1,)), ((), ())), prefe...  18.9 us
    dot_general x1, matrix products, local(): jnp.einsum('jcr,jcs->crs', centered, centered, precision=highest)  16.8 us
  transfers between devices with their start and end apart: 1, of which 1 were waited for; matrix products, arithmetic and copies ran while one was open for 2% of the time, Pallas kernels for 0%

profile of v1, /device:TPU:0, one launch (start us, length us, event | category | flops | bytes accessed | tf_op | source)
XLA Modules:
  0.0 655.4 jit_solution(5738952224861552890)
XLA Ops:
  7.2 11.9 %copy.9 = bf16[512,8192]{0,1:T(8,128)(2,1)} copy(bf16[512,8192]{1,0:T(8,128)(2,1)} %param.4) | data formatting | bytes 16777216 | tf_op args[1]
  19.1 12.3 %copy.10 = bf16[512,16,512]{2,0,1:T(8,128)(2,1)} copy(bf16[512,16,512]{0,2,1:T(8,128)(2,1)} %bitcast.35) | data formatting | bytes 16777216 | tf_op jit(solution)/shard_map/all_to_all | solution.py:31
  31.4 103.2 %all_to_all.33 = bf16[512,16,512]{2,0,1:T(8,128)(2,1)} all-to-all(bf16[512,16,512]{2,0,1:T(8,128)(2,1)} %copy.10), channel_id=1, replica_groups=mesh['dp_0'=4,'dp_1'=2,'mp_0'=4,'mp_1'=4] {'mp_0','mp_1'}, dimensions={1} | all-to-all | bytes 16777216 | tf_op jit(solution)/shard_map/all_to_all | solution.py:31
  134.6 2.9 stack.12
  137.5 281.0 %all_to_all.34 = bf16[16,8,192,512]{3,2,1,0:T(8,128)(2,1)} all-to-all(bf16[16,8,192,512]{3,2,1,0:T(8,128)(2,1)S(1)} %stack.12), channel_id=1, replica_groups=mesh['dp_0'=4,'dp_1'=2,'mp_0'=4,'mp_1'=4] {'mp_0','mp_1'}, dimensions={0} | all-to-all | bytes 50331648 | tf_op jit(solution)/shard_map/all_to_all | solution.py:20
  418.5 18.9 %fusion.5 = f32[512,8,192]{0,2,1:T(8,128)S(1)} fusion(bf16[16,8,192,512]{3,2,1,0:T(8,128)(2,1)} %all_to_all.34, bf16[512,16,512]{2,0,1:T(8,128)(2,1)} %all_to_all.33), kind=kOutput, calls=%fused_computation.10 | convolution fusion | flops 12884901888 | bytes 36700160 | tf_op jit(solution)/shard_map/dot_general | solution.py:34
  437.4 1.7 copy-done
  439.1 43.5 %all_to_all.35 = f32[512,8,192]{0,2,1:T(8,128)S(1)} all-to-all(f32[512,8,192]{0,2,1:T(8,128)S(1)} %fusion.5), channel_id=1, replica_groups=mesh['dp_0'=4,'dp_1'=2,'mp_0'=4,'mp_1'=4] {'dp_0','dp_1'}, dimensions={1} | all-to-all | bytes 6291456 | tf_op jit(solution)/shard_map/all_to_all | solution.py:47
  482.6 0.3 reduce_sum.65
  482.9 0.6 multiply_reduce_fusion.1
  483.4 16.8 %fusion.4 = bf16[1,1536,1536]{2,1,0:T(8,128)(2,1)} fusion(f32[512,1536]{0,1:T(8,128)S(1)} %bitcast.36), kind=kOutput, calls=%fused_computation.6 | convolution fusion | flops 14497873920 | bytes 7864320 | tf_op jit(solution)/shard_map/jcr,jcs->crs/dot_general | solution.py:55
  500.2 0.7 copy-done.2
  500.9 3.9 convolution_bitcast_fusion
  504.8 0.1 slice_bitcast_fusion.1
  504.9 2.0 multiply_reduce_fusion.2
  508.1 5.4 copy.12
  513.6 0.7 multiply_reduce_fusion.4
  514.2 89.2 %all-reduce.6.cloned.1.call-done = bf16[1,1536,1536]{2,1,0:T(8,128)(2,1)} async-done(((bf16[1,1536,1536]{2,1,0:T(8,128)(2,1)}), bf16[1,1536,1536]{2,1,0:T(8,128)(2,1)}) %all-reduce.6.cloned.1.call-update) | async-done | bytes 4718608 | tf_op jit(solution)/shard_map/psum | solution.py:56
  603.4 5.3 multiply_reduce_fusion
  610.0 11.3 %all-reduce.2 = (f32[]{:T(128)}, f32[]{:T(128)}, f32[]{:T(128)}) all-reduce(f32[]{:T(128)S(6)} %add.47, f32[]{:T(128)} %get-tuple-element.11, f32[]{:T(128)S(6)} %sub.61), channel_id=1, replica_groups=mesh['dp_0'=4,'dp_1'=2,'mp_0'=4,'mp_1'=4] {'dp_0'}, use_global_device_ids=true, to_apply=%region_2.0 | all-reduce | flops 3 | bytes 24 | tf_op jit(solution)/shard_map/psum | solution.py:24
  621.2 3.2 all-reduce.3
  624.4 11.0 %all-reduce.1 = (f32[]{:T(128)}, f32[]{:T(128)}, f32[]{:T(128)}) all-reduce(f32[]{:T(128)} %get-tuple-element.21, f32[]{:T(128)} %get-tuple-element.22, f32[]{:T(128)} %get-tuple-element.23), channel_id=1, replica_groups=mesh['dp_0'=4,'dp_1'=2,'mp_0'=4,'mp_1'=4] {'mp_0'}, use_global_device_ids=true, to_apply=%region_4.5 | all-reduce | flops 3 | bytes 24 | tf_op jit(solution)/shard_map/psum | solution.py:24
  635.3 9.4 %all-reduce = (f32[]{:T(128)}, f32[]{:T(128)}, f32[]{:T(128)}) all-reduce(f32[]{:T(128)} %get-tuple-element.15, f32[]{:T(128)} %get-tuple-element.16, f32[]{:T(128)} %get-tuple-element.17), channel_id=1, replica_groups=mesh['dp_0'=4,'dp_1'=2,'mp_0'=4,'mp_1'=4] {'mp_1'}, use_global_device_ids=true, to_apply=%region_5.6 | all-reduce | flops 3 | bytes 24 | tf_op jit(solution)/shard_map/psum | solution.py:24
  647.9 0.6 pad_maximum_fusion
  (7 shorter events, 0.1 us)
Async XLA Ops:
  7.2 596.2 %all-reduce.6.cloned.1.call-start = ((), (), s32[]{:S(2)}) async-start(), calls=%async_computation.3 | async-start | bytes 9437184 | tf_op jit(solution)/shard_map/psum | solution.py:56
  31.4 103.2 %copy-start.1 = (bf16[8,192,512]{2,1,0:T(8,128)(2,1)S(1)}, bf16[8,192,512]{2,1,0:T(8,128)(2,1)}, u32[]{:S(2)}) copy-start(bf16[8,192,512]{2,1,0:T(8,128)(2,1)} %param.3) | copy-start | bytes 4718596
  437.4 1.7 copy-start
  500.2 0.7 copy-start.2
Sparse Core Ops, SparseCore 0:
  500.3 103.0 all-reduce.5
